TPU v7x, 32 devices: a whole 2x2x4 slice. The times are simulated.
32 devices in a mesh: section: 2 (over core), seq: 4 (over y, x), mp: 4 (over z).
Axes of the slice: x: 2, y: 2, z: 4, core: 2. Of those that a mesh axis runs over, the one named last changes fastest.
Arguments:
- token_ids: int32 [2, 1024], P(None, 'seq'), may hold values from 0 to 511
- embed_table: bfloat16 [512, 4096], P(None, 'mp'), may hold values from -40 to 40
- norm_gain: bfloat16 [2, 4096], P('section', 'mp'), may hold values from 0.099609375 to 1.8984375
- short_filters: bfloat16 [2, 3, 7, 4096], P('section', None, None, 'mp'), may hold values from -2 to 2
- medium_filters: bfloat16 [2, 128, 4096], P('section', None, 'mp'), may hold values from -0.5 to 0.5
- out_weight: bfloat16 [2, 4096, 4096], P('section', 'seq', 'mp'), may hold values from -0.09375 to 0.09375
Outputs:
- streams: bfloat16 [2, 2, 1024, 4096], P('section', None, 'seq', 'mp')
All inputs are finite; a program needn't handle non-finite values.
Results may differ from a plain program's by a relative error of at most 0.018.
Values may be sent and summed in bfloat16 or wider, within the bound.
A program may use at most 64 MiB of HBM per device.

v0:
```python
import jax
import jax.numpy as jnp
from jax import lax
from jax.sharding import PartitionSpec as P

D = 4096


def passed_along(value, axis, by):
    devices = lax.axis_size(axis)
    pairs = [(i, i + by) for i in range(devices) if 0 <= i + by < devices]
    return lax.ppermute(value, axis, pairs)


def depthwise(extended, taps):
    kernel = jnp.flip(taps, 0)[:, None, :]
    result = lax.conv_general_dilated(
        extended[None],
        kernel,
        (1,),
        "VALID",
        dimension_numbers=("NWC", "WIO", "NWC"),
        feature_group_count=taps.shape[1],
        preferred_element_type=jnp.float32,
    )
    return result[0]


def mixer_layer(stream_in, gain, shorts, medium, weight_cols):
    rows = stream_in.shape[0]
    stream = stream_in.astype(jnp.float32)
    own_squares = jnp.sum(stream * stream, axis=1, keepdims=True)
    all_squares = lax.psum(own_squares, "mp")
    normed = (
        stream * lax.rsqrt(all_squares / D + 1e-06) * gain.astype(jnp.float32)[None, :]
    ).astype(jnp.bfloat16)
    short_span = shorts.shape[1] - 1
    medium_span = medium.shape[0] - 1
    lower_rim = passed_along(normed[rows - short_span :], "seq", 1)
    extended = jnp.concatenate([lower_rim, normed], axis=0)
    features = [depthwise(extended, shorts[index]).astype(jnp.bfloat16) for index in range(3)]
    product = (features[1].astype(jnp.float32) * features[2].astype(jnp.float32)).astype(
        jnp.bfloat16
    )
    product_rim = passed_along(product[rows - medium_span :], "seq", 1)
    filtered = depthwise(jnp.concatenate([product_rim, product], axis=0), medium)
    query = features[0]
    gated = (query.astype(jnp.float32) * filtered).astype(jnp.bfloat16)
    empty = jnp.zeros((rows, weight_cols.shape[1]), jnp.float32)
    piece = jax.tree.map(lambda a: lax.all_gather(a, "mp", axis=1, tiled=True), gated)
    block_rows = lax.slice_in_dim(weight_cols, 0, piece.shape[1], axis=0)
    projected = empty + jnp.dot(piece, block_rows, preferred_element_type=jnp.float32)
    return (stream + projected).astype(jnp.bfloat16)


def local(token_ids, embed_table, norm_gain, short_filters, medium_filters, out_weight):
    section_index = lax.axis_index("section")
    weight_cols = lax.all_gather(out_weight, "seq", axis=1, tiled=True)[0]
    gain = norm_gain[0]
    shorts = short_filters[0]
    medium = medium_filters[0]
    micro_count = token_ids.shape[0]
    rows = token_ids.shape[1]
    width = embed_table.shape[1]
    vocab_ids = lax.broadcasted_iota(jnp.int32, (rows, embed_table.shape[0]), 1)
    received = jnp.zeros((rows, width), jnp.bfloat16)
    results = []
    for tick_index in range(micro_count + 1):
        chosen = token_ids[min(tick_index, micro_count - 1)]
        one_hot = (chosen[:, None] == vocab_ids).astype(jnp.bfloat16)
        embedded = jnp.dot(one_hot, embed_table, preferred_element_type=jnp.float32).astype(
            jnp.bfloat16
        )
        stream_in = jnp.where(section_index == 0, embedded, received)
        result = mixer_layer(stream_in, gain, shorts, medium, weight_cols)
        results.append(result)
        if tick_index < micro_count:
            received = passed_along(result, "section", 1)
    ordered = [
        jnp.where(section_index == 0, results[index], results[index + 1])
        for index in range(micro_count)
    ]
    return jnp.stack(ordered)[None]


def solution(mesh):
    in_specs = (
        P(None, "seq"),
        P(None, "mp"),
        P("section", "mp"),
        P("section", None, None, "mp"),
        P("section", None, "mp"),
        P("section", "seq", "mp"),
    )
    out_specs = P("section", None, "seq", "mp")
    return jax.shard_map(local, mesh=mesh, in_specs=in_specs, out_specs=out_specs, check_vma=False)
```

profile of v0, /device:TPU:0, one launch (start us, length us, event | category | flops | bytes accessed | tf_op | source)
XLA Modules:
  0.0 514.0 jit_solution(5375181700684785683)
XLA Ops:
  6.5 0.8 fusion.139
  7.3 0.7 mul.112
  8.6 13.5 %psum.21 = f32[256,1]{0,1:T(1,128)S(1)} all-reduce(f32[256,1]{0,1:T(1,128)S(1)} %bitcast.136), channel_id=1, replica_groups=mesh['section'=2,'seq'=4,'mp'=4] {'mp'}, use_global_device_ids=true, to_apply=%region_1.2 | all-reduce | flops 256 | bytes 2048 | tf_op jit(solution)/shard_map/psum | solution.py:33
  22.3 3.4 collective-permute-start
  26.5 2.6 rev.25
  30.6 0.7 fusion.23
  31.7 0.8 slice_bitcast_fusion.5
  32.5 4.1 collective-permute-start.1
  37.2 0.6 copy.28
  37.9 2.3 reshape.126
  40.2 1.2 maximum_bitcast_fusion.1
  41.5 15.2 %fusion.86 = bf16[1,256,1024]{2,0,1:T(2,128)(2,1)} fusion(bf16[1,383,1024]{2,1,0:T(8,128)(2,1)S(1)} %maximum_bitcast_fusion.1, f32[1,264,1024]{2,0,1:T(1,128)S(1)} %copy-done.2, bf16[128,1,1024]{2,0,1:T(8,128)(2,1)S(1)} %bitcast.116), kind=kOutput, calls=%fused_computation.73 | convolution fusion | flops 67633152 | bytes 2619392 | tf_op jit(solution)/shard_map/conv_general_dilated | solution.py:17
  56.7 0.7 all-gather.8.cloned.1.call-update
  58.0 78.3 %all-gather.10.cloned.1.call-done = bf16[1,256,4096]{2,0,1:T(2,128)(2,1)} async-done(((bf16[1,256,1024]{2,0,1:T(2,128)(2,1)}), bf16[1,256,4096]{2,0,1:T(2,128)(2,1)}) %all-gather.10.cloned.1.call-update) | async-done | bytes 2097168 | tf_op jit(solution)/shard_map/all_gather | solution.py:50
  136.3 87.5 %all-gather.8.cloned.1.call-done = bf16[1,4096,1024]{2,1,0:T(8,128)(2,1)} async-done(((bf16[1,1024,1024]{2,1,0:T(8,128)(2,1)}), bf16[1,4096,1024]{2,1,0:T(8,128)(2,1)}) %all-gather.8.cloned.1.call-update) | async-done | bytes 8388624 | tf_op jit(solution)/shard_map/all_gather | solution.py:58
  223.8 8.6 %fusion.54 = bf16[256,1024]{1,0:T(8,128)(2,1)S(1)} fusion(bf16[1,4096,1024]{2,1,0:T(8,128)(2,1)} %all-gather.8.cloned.1.call-done, bf16[1,256,4096]{2,0,1:T(2,128)(2,1)} %all-gather.10.cloned.1.call-done, bf16[256,1024]{1,0:T(8,128)(2,1)S(1)} %get-tuple-element.15), kind=kOutput, calls=%fused_computation.62 | convolution fusion | flops 2148270080 | bytes 11534336 | tf_op jit(solution)/shard_map/dot_general | solution.py:52
  232.5 1.6 collective-permute-start.2
  234.1 1.5 collective-permute-done.2
  236.2 11.7 %psum.22 = f32[256,1]{0,1:T(1,128)S(1)} all-reduce(f32[256,1]{0,1:T(1,128)S(1)} %bitcast.135), channel_id=1, replica_groups=mesh['section'=2,'seq'=4,'mp'=4] {'mp'}, use_global_device_ids=true, to_apply=%region_3.4 | all-reduce | flops 256 | bytes 2048 | tf_op jit(solution)/shard_map/psum | solution.py:33
  248.1 3.4 collective-permute-start.3
  251.5 1.4 collective-permute-done.3
  254.2 0.7 fusion.31
  255.4 0.8 slice_bitcast_fusion.4
  256.2 4.9 collective-permute-start.4
  261.7 0.6 copy.38
  262.3 1.3 reshape.127
  263.7 0.9 collective-permute-done.4
  264.6 1.1 maximum_bitcast_fusion.2
  265.7 15.2 %fusion.92 = bf16[1,256,1024]{2,0,1:T(2,128)(2,1)} fusion(bf16[1,383,1024]{2,1,0:T(8,128)(2,1)S(1)} %maximum_bitcast_fusion.2, f32[1,264,1024]{2,0,1:T(1,128)S(1)} %reshape.127, bf16[128,1,1024]{2,0,1:T(8,128)(2,1)S(1)} %bitcast.117), kind=kOutput, calls=%fused_computation.75 | convolution fusion | flops 67633152 | bytes 2619392 | tf_op jit(solution)/shard_map/conv_general_dilated | solution.py:17
  281.1 80.5 %all-gather.12.cloned.1.call-done = bf16[1,256,4096]{2,0,1:T(2,128)(2,1)} async-done(((bf16[1,256,1024]{2,0,1:T(2,128)(2,1)}), bf16[1,256,4096]{2,0,1:T(2,128)(2,1)}) %all-gather.12.cloned.1.call-update) | async-done | bytes 2097168 | tf_op jit(solution)/shard_map/all_gather | solution.py:50
  361.6 8.6 %fusion.59 = bf16[256,1024]{1,0:T(8,128)(2,1)S(1)} fusion(bf16[1,4096,1024]{2,1,0:T(8,128)(2,1)} %all-gather.8.cloned.1.call-done, bf16[1,256,4096]{2,0,1:T(2,128)(2,1)} %all-gather.12.cloned.1.call-done, bf16[256,1024]{1,0:T(8,128)(2,1)S(1)} %copy-done.4), kind=kOutput, calls=%fused_computation.63 | convolution fusion | flops 2148270080 | bytes 11534336 | tf_op jit(solution)/shard_map/dot_general | solution.py:52
  370.2 1.3 collective-permute-start.5
  371.6 1.5 collective-permute-done.5
  373.3 9.4 %psum.23 = f32[256,1]{0,1:T(1,128)S(1)} all-reduce(f32[256,1]{0,1:T(1,128)S(1)} %bitcast.131), channel_id=1, replica_groups=mesh['section'=2,'seq'=4,'mp'=4] {'mp'}, use_global_device_ids=true, to_apply=%region_5.6 | all-reduce | flops 256 | bytes 2048 | tf_op jit(solution)/shard_map/psum | solution.py:33
  382.9 3.4 collective-permute-start.6
  386.3 1.4 collective-permute-done.6
  389.1 0.7 fusion.39
  390.2 0.8 slice_bitcast_fusion.3
  391.0 5.1 collective-permute-start.7
  396.7 0.6 copy.48
  397.4 1.3 reshape.128
  398.7 0.7 collective-permute-done.7
  399.4 1.1 maximum_bitcast_fusion.3
  400.5 15.2 %fusion.98 = bf16[1,256,1024]{2,0,1:T(2,128)(2,1)} fusion(bf16[1,383,1024]{2,1,0:T(8,128)(2,1)S(1)} %maximum_bitcast_fusion.3, f32[1,264,1024]{2,0,1:T(1,128)S(1)} %reshape.128, bf16[128,1,1024]{2,0,1:T(8,128)(2,1)S(1)} %bitcast.118), kind=kOutput, calls=%fused_computation.77 | convolution fusion | flops 67633152 | bytes 2619392 | tf_op jit(solution)/shard_map/conv_general_dilated | solution.py:17
  415.7 1.0 copy-done.6
  416.9 80.5 %all-gather.14.cloned.1.call-done = bf16[1,256,4096]{2,0,1:T(2,128)(2,1)} async-done(((bf16[1,256,1024]{2,0,1:T(2,128)(2,1)}), bf16[1,256,4096]{2,0,1:T(2,128)(2,1)}) %all-gather.14.cloned.1.call-update) | async-done | bytes 2097168 | tf_op jit(solution)/shard_map/all_gather | solution.py:50
  497.4 8.7 %fusion.78 = bf16[1,256,1024]{2,1,0:T(8,128)(2,1)S(1)} fusion(bf16[256,1024]{1,0:T(8,128)(2,1)S(1)} %copy-done.8, bf16[1,4096,1024]{2,1,0:T(8,128)(2,1)} %all-gather.8.cloned.1.call-done, bf16[1,256,4096]{2,0,1:T(2,128)(2,1)} %all-gather.14.cloned.1.call-done, bf16[256,1024]{1,0:T(8,128)(2,1)S(1)} %get-tuple-element.6, pred[]{:T(512)S(6)} %eq.14), kind=kOutput, calls=%fused_computation.71 | convolution fusion | flops 2148532224 | bytes 12058625 | tf_op jit(solution)/shard_map/dot_general | solution.py:52
  506.1 1.1 maximum_bitcast_fusion
  (85 shorter events, 11.3 us)
Async XLA Ops:
  6.5 1.5 copy-start
  6.5 129.7 %all-gather.10.cloned.1.call-start = ((), (), s32[]{:S(2)}) async-start(), calls=%async_computation.1 | async-start | bytes 5242880 | tf_op jit(solution)/shard_map/all_gather | solution.py:50
  8.0 17.7 %copy-start.13 = (bf16[1,3,7,1024]{3,2,1,0:T(8,128)(2,1)S(1)}, bf16[1,3,7,1024]{3,2,1,0:T(8,128)(2,1)}, u32[]{:S(2)}) copy-start(bf16[1,3,7,1024]{3,2,1,0:T(8,128)(2,1)} %param.9) | copy-start | bytes 129028
  8.0 18.5 %copy-start.9 = (bf16[1,128,1024]{2,1,0:T(8,128)(2,1)S(1)}, bf16[1,128,1024]{2,1,0:T(8,128)(2,1)}, u32[]{:S(2)}) copy-start(bf16[1,128,1024]{2,1,0:T(8,128)(2,1)} %param.10) | copy-start | bytes 786436
  22.3 6.8 %collective-permute-start = (bf16[6,1024]{1,0:T(8,128)(2,1)S(1)}, bf16[6,1024]{1,0:T(8,128)(2,1)S(1)}, u32[]{:S(2)}, u32[]{:S(2)}) collective-permute-start(bf16[6,1024]{1,0:T(8,128)(2,1)S(1)} %slice.84), channel_id=1, source_target_pairs={{0,4},{4,8},{8,12},{1,5},{5,9},{9,13},{2,6},{6,10},{10,14},{3,7},{... | collective-permute-start | bytes 36872 | tf_op jit(solution)/shard_map/ppermute | solution.py:12
  29.3 0.7 copy-start.14
  32.5 7.7 %collective-permute-start.1 = (bf16[127,1024]{1,0:T(8,128)(2,1)}, bf16[127,1024]{1,0:T(8,128)(2,1)}, u32[]{:S(2)}, u32[]{:S(2)}) collective-permute-start(bf16[127,1024]{1,0:T(8,128)(2,1)} %slice_bitcast_fusion.5), channel_id=1, source_target_pairs={{0,4},{4,8},{8,12},{1,5},{5,9},{9,13},{2,6},{6,10},{10,14},{3,7},{... | collective-permute-start | bytes 780296 | tf_op jit(solution)/shard_map/ppermute | solution.py:12
  40.2 1.3 copy-start.2
  40.2 1.4 copy-start.10
  56.7 167.1 %all-gather.8.cloned.1.call-start = ((), (), s32[]{:S(2)}) async-start(), calls=%async_computation | async-start | bytes 10485760 | tf_op jit(solution)/shard_map/all_gather | solution.py:58
  57.5 304.1 %all-gather.12.cloned.1.call-start = ((), (), s32[]{:S(2)}) async-start(), calls=%async_computation.2 | async-start | bytes 5242880 | tf_op jit(solution)/shard_map/all_gather | solution.py:50
  232.5 3.1 copy-start.5
  232.5 3.1 collective-permute-start.2
  236.2 16.7 %copy-start.3 = (bf16[256,1024]{1,0:T(8,128)(2,1)}, bf16[256,1024]{1,0:T(8,128)(2,1)S(1)}, u32[]{:S(2)}) copy-start(bf16[256,1024]{1,0:T(8,128)(2,1)S(1)} %get-tuple-element.8) | copy-start | bytes 1572868
  248.1 4.8 collective-permute-start.3
  256.2 8.4 %collective-permute-start.4 = (bf16[127,1024]{1,0:T(8,128)(2,1)}, bf16[127,1024]{1,0:T(8,128)(2,1)}, u32[]{:S(2)}, u32[]{:S(2)}) collective-permute-start(bf16[127,1024]{1,0:T(8,128)(2,1)} %slice_bitcast_fusion.4), channel_id=1, source_target_pairs={{0,4},{4,8},{8,12},{1,5},{5,9},{9,13},{2,6},{6,10},{10,14},{3,7},{... | collective-permute-start | bytes 780296 | tf_op jit(solution)/shard_map/ppermute | solution.py:12
  263.6 2.0 copy-start.11
  265.6 95.9 %copy-start.4 = (bf16[256,1024]{1,0:T(8,128)(2,1)S(1)}, bf16[256,1024]{1,0:T(8,128)(2,1)}, u32[]{:S(2)}) copy-start(bf16[256,1024]{1,0:T(8,128)(2,1)} %copy-done.3) | copy-start | bytes 1572868
  280.9 216.5 %all-gather.14.cloned.1.call-start = ((), (), s32[]{:S(2)}) async-start(), calls=%async_computation.3 | async-start | bytes 5242880 | tf_op jit(solution)/shard_map/all_gather | solution.py:50
  370.2 12.7 %copy-start.7 = (bf16[256,1024]{1,0:T(8,128)(2,1)}, bf16[256,1024]{1,0:T(8,128)(2,1)S(1)}, u32[]{:S(2)}) copy-start(bf16[256,1024]{1,0:T(8,128)(2,1)S(1)} %fusion.59) | copy-start | bytes 1572868
  370.2 2.8 collective-permute-start.5
  382.9 4.8 collective-permute-start.6
  391.0 8.4 %collective-permute-start.7 = (bf16[127,1024]{1,0:T(8,128)(2,1)}, bf16[127,1024]{1,0:T(8,128)(2,1)}, u32[]{:S(2)}, u32[]{:S(2)}) collective-permute-start(bf16[127,1024]{1,0:T(8,128)(2,1)} %slice_bitcast_fusion.3), channel_id=1, source_target_pairs={{0,4},{4,8},{8,12},{1,5},{5,9},{9,13},{2,6},{6,10},{10,14},{3,7},{... | collective-permute-start | bytes 780296 | tf_op jit(solution)/shard_map/ppermute | solution.py:12
  398.7 1.8 copy-start.12
  415.7 1.0 copy-start.6
  415.7 1.2 copy-start.8
  497.4 9.8 %copy-start.1 = (bf16[512,1024]{1,0:T(8,128)(2,1)S(1)}, bf16[512,1024]{1,0:T(8,128)(2,1)}, u32[]{:S(2)}) copy-start(bf16[512,1024]{1,0:T(8,128)(2,1)} %param.7) | copy-start | bytes 3145732
Sparse Core Ops, SparseCore 0:
  56.8 79.4 all-gather.9
  138.1 85.6 all-gather.7
  281.0 80.5 all-gather.11
  415.8 81.5 all-gather.13
where the time goes:
time: 521 us; the launch traced here: 514 us
  waiting for transfers between devices  335 us (64%)
  matrix products  78.3 us (15%)
  blocking collectives  34.5 us (7%)
  starting transfers between devices  27.9 us (5%)
  local copies, waits for them, and re-layouts  18 us (3%)
  between operations  13.9 us (3%)
  other arithmetic  6.4 us (1%)
    all_gather x3, waiting for transfers between devices, mixer_layer(): lax.all_gather(a, 'mp', axis=1, tiled=True)  239 us
    all_gather x1, waiting for transfers between devices, local(): weight_cols = lax.all_gather(out_weight, 'seq', axis=1, tiled=True)[0]  87.5 us
    conv_general_dilated x12, matrix products, depthwise(): lax.conv_general_dilated(extended[None], kernel, (1,), 'VALID', dimension...  51.1 us
    psum x3, blocking collectives, mixer_layer(): all_squares = lax.psum(own_squares, 'mp')  34.5 us
    ppermute x8, starting transfers between devices, passed_along(): return lax.ppermute(value, axis, pairs)  27.2 us
    dot_general x3, matrix products, mixer_layer(): jnp.dot(piece, block_rows, preferred_element_type=jnp.float32)  26 us
  transfers between devices with their start and end apart: 12, of which 10 were waited for; matrix products, arithmetic and copies ran while one was open for 2% of the time, Pallas kernels for 0%

commit v1 on v0

--- a/solution.py
+++ b/solution.py
@@ -4,6 +4,28 @@
 from jax.sharding import PartitionSpec as P
 
 D = 4096
+
+
+def laid_out(blocks, dim):
+    blocks = jnp.moveaxis(blocks, 0, dim)
+    shape = blocks.shape
+    return blocks.reshape(*shape[:dim], shape[dim] * shape[dim + 1], *shape[dim + 2 :])
+
+
+def grow_blocks(x, axis):
+    count = lax.axis_size(axis)
+    blocks = x[None]
+    for level in range(count.bit_length() - 1):
+        bit = 1 << level
+        received = lax.ppermute(blocks, axis, [(i, i ^ bit) for i in range(count)])
+        both = jnp.stack([blocks, received])
+        upper = lax.axis_index(axis) >> level & 1
+        blocks = jnp.where(upper == 0, both, both[::-1]).reshape(-1, *x.shape)
+    return blocks
+
+
+def doubled_up(value, axis, dim):
+    return laid_out(grow_blocks(value, axis), dim)
 
 
 def passed_along(value, axis, by):
@@ -55,7 +77,7 @@
 
 def local(token_ids, embed_table, norm_gain, short_filters, medium_filters, out_weight):
     section_index = lax.axis_index("section")
-    weight_cols = lax.all_gather(out_weight, "seq", axis=1, tiled=True)[0]
+    weight_cols = doubled_up(out_weight, "seq", 1)[0]
     gain = norm_gain[0]
     shorts = short_filters[0]
     medium = medium_filters[0]

time: 521 us -> 482 us (0.925)
  waiting for transfers between devices: 335 us -> 264 us
  other arithmetic: 6.4 us -> 34.3 us
    all_gather x1 -> x0, waiting for transfers between devices: 87.5 us -> none  [local(): weight_cols = lax.all_gather(out_weight, 'seq', axis=1, tiled=True)[0]]
    all_gather x3, waiting for transfers between devices: 239 us -> 161 us  [mixer_layer(): lax.all_gather(a, 'mp', axis=1, tiled=True)]
    ppermute x0 -> x2, waiting for transfers between devices: none -> 70.7 us  [grow_blocks(): received = lax.ppermute(blocks, axis, [(i, i ^ bit) for i in range(count)])]
    ppermute x8, waiting for transfers between devices: 7.38 us -> 31.6 us  [passed_along(): return lax.ppermute(value, axis, pairs)]
    another operation x0 -> x3, other arithmetic: none -> 14.3 us  [grow_blocks(): both = jnp.stack([blocks, received])]
    select_n x0 -> x1, other arithmetic: none -> 13.5 us  [grow_blocks(): blocks = jnp.where(upper == 0, both, both[::-1]).reshape(-1, *x.shape)]
  transfers between devices with their start and end apart: 12 -> 13, of which waited for: 10 -> 9; matrix products, arithmetic and copies ran while one was open for 2% -> 13% of each run, Pallas kernels for 0% -> 0%
where the time goes in v1:
time: 482 us; the launch traced here: 475 us
  waiting for transfers between devices  264 us (55%)
  matrix products  79 us (16%)
  other arithmetic  34.3 us (7%)
  blocking collectives  33.4 us (7%)
  starting transfers between devices  30.3 us (6%)
  local copies, waits for them, and re-layouts  20 us (4%)
  between operations  13.9 us (3%)
    all_gather x3, waiting for transfers between devices, mixer_layer(): lax.all_gather(a, 'mp', axis=1, tiled=True)  161 us
    ppermute x2, waiting for transfers between devices, grow_blocks(): received = lax.ppermute(blocks, axis, [(i, i ^ bit) for i in range(count)])  70.7 us
    conv_general_dilated x12, matrix products, depthwise(): lax.conv_general_dilated(extended[None], kernel, (1,), 'VALID', dimension...  51.1 us
    psum x3, blocking collectives, mixer_layer(): all_squares = lax.psum(own_squares, 'mp')  33.4 us
    ppermute x8, waiting for transfers between devices, passed_along(): return lax.ppermute(value, axis, pairs)  31.6 us
    dot_general x3, matrix products, mixer_layer(): jnp.dot(piece, block_rows, preferred_element_type=jnp.float32)  26 us
    ppermute x8, starting transfers between devices, passed_along(): return lax.ppermute(value, axis, pairs)  26 us
    another operation x3, other arithmetic, grow_blocks(): both = jnp.stack([blocks, received])  14.3 us
  transfers between devices with their start and end apart: 13, of which 9 were waited for; matrix products, arithmetic and copies ran while one was open for 13% of the time, Pallas kernels for 0%

profile of v1, /device:TPU:0, one launch (start us, length us, event | category | flops | bytes accessed | tf_op | source)
XLA Modules:
  0.0 474.6 jit_solution(5921552609799342904)
XLA Ops:
  6.5 3.0 collective-permute-start.2
  9.5 0.8 fusion.122
  10.3 0.7 mul.112
  11.5 12.1 %psum.21 = f32[256,1]{0,1:T(1,128)S(1)} all-reduce(f32[256,1]{0,1:T(1,128)S(1)} %bitcast.130), channel_id=1, replica_groups=mesh['section'=2,'seq'=4,'mp'=4] {'mp'}, use_global_device_ids=true, to_apply=%region_1.2 | all-reduce | flops 256 | bytes 2048 | tf_op jit(solution)/shard_map/psum | solution.py:55
  23.9 2.4 collective-permute-start
  27.1 2.6 rev.31
  29.7 25.3 %collective-permute-done = bf16[6,1024]{1,0:T(8,128)(2,1)S(1)} collective-permute-done((bf16[6,1024]{1,0:T(8,128)(2,1)S(1)}, bf16[6,1024]{1,0:T(8,128)(2,1)S(1)}, u32[]{:S(2)}, u32[]{:S(2)}) %collective-permute-start) | collective-permute-done | bytes 12320 | tf_op jit(solution)/shard_map/ppermute | solution.py:34
  57.6 0.8 slice_bitcast_fusion.5
  58.4 5.1 %collective-permute-start.1 = (bf16[127,1024]{1,0:T(8,128)(2,1)}, bf16[127,1024]{1,0:T(8,128)(2,1)}, u32[]{:S(2)}, u32[]{:S(2)}) collective-permute-start(bf16[127,1024]{1,0:T(8,128)(2,1)} %slice_bitcast_fusion.5), channel_id=1, source_target_pairs={{0,4},{4,8},{8,12},{1,5},{5,9},{9,13},{2,6},{6,10},{10,14},{3,7},{... | collective-permute-start | bytes 780296 | tf_op jit(solution)/shard_map/ppermute | solution.py:34
  64.1 1.0 copy-done.2
  65.1 2.0 pad_maximum_fusion.1
  67.0 4.9 %fusion.1 = (bf16[1,2,1,1024,1024]{4,3,1,2,0:T(8,128)(2,1)}, bf16[2,1,1024,1024]{3,2,0,1:T(8,128)(2,1)}) fusion(bf16[2,1,1,1024,1024]{4,3,2,1,0:T(8,128)(2,1)S(1)} %pad_maximum_fusion.1, pred[]{:T(512)S(6)} %eq.42), kind=kLoop, calls=%fused_computation.5 | loop fusion | flops 2097152 | bytes 12582913 | tf_op jit(solution)/shard_map/stack;reshape | solution.py:21
  72.0 0.8 collective-permute-start.3
  73.5 2.3 reshape.130
  75.8 1.2 maximum_bitcast_fusion.1
  77.2 15.2 %fusion.69 = bf16[1,256,1024]{2,0,1:T(2,128)(2,1)} fusion(bf16[1,383,1024]{2,1,0:T(8,128)(2,1)S(1)} %maximum_bitcast_fusion.1, f32[1,264,1024]{2,0,1:T(1,128)S(1)} %copy-done.4, bf16[128,1,1024]{2,0,1:T(8,128)(2,1)S(1)} %bitcast.110), kind=kOutput, calls=%fused_computation.76 | convolution fusion | flops 67633152 | bytes 2619392 | tf_op jit(solution)/shard_map/conv_general_dilated | solution.py:39
  92.9 70.7 %collective-permute-done.3 = bf16[2,1,1024,1024]{3,2,0,1:T(8,128)(2,1)} collective-permute-done((bf16[2,1,1024,1024]{3,2,0,1:T(8,128)(2,1)}, bf16[2,1,1024,1024]{3,2,0,1:T(8,128)(2,1)}, u32[]{:S(2)}, u32[]{:S(2)}) %collective-permute-start.3) | collective-permute-done | bytes 4194336 | tf_op jit(solution)/shard_map/ppermute | solution.py:20
  163.6 7.4 %pad_maximum_fusion = bf16[2,2,1,1024,1024]{4,3,1,2,0:T(8,128)(2,1)} fusion(bf16[1,2,1,1024,1024]{4,3,1,2,0:T(8,128)(2,1)} %bitcast.22, bf16[1,2,1,1024,1024]{4,3,1,2,0:T(8,128)(2,1)} %get-tuple-element.9), kind=kLoop, calls=%fused_computation.1 | loop fusion | flops 4194304 | bytes 16777216 | tf_op jit(solution)/shard_map/stack | solution.py:21
  171.0 13.5 %reverse_select_fusion = bf16[2,2,1,1024,1024]{4,3,1,2,0:T(8,128)(2,1)} fusion(bf16[2,2,1,1024,1024]{4,3,1,2,0:T(8,128)(2,1)} %pad_maximum_fusion, pred[]{:T(512)S(6)} %eq.41), kind=kLoop, calls=%fused_computation | loop fusion | flops 4194304 | bytes 16777216 | tf_op jit(solution)/shard_map/jit(_where)/select_n | solution.py:23
  184.5 8.6 %fusion.47 = bf16[256,1024]{1,0:T(8,128)(2,1)S(1)} fusion(bf16[4096,1024]{1,0:T(8,128)(2,1)} %bitcast.104, bf16[1,256,4096]{2,0,1:T(2,128)(2,1)} %all-gather.7.cloned.1.call-done, bf16[256,1024]{1,0:T(8,128)(2,1)S(1)} %get-tuple-element.17), kind=kOutput, calls=%fused_computation.65 | convolution fusion | flops 2148270080 | bytes 11534336 | tf_op jit(solution)/shard_map/dot_general | solution.py:74
  193.1 1.3 collective-permute-start.4
  194.5 1.5 collective-permute-done.4
  196.0 1.3 fusion.87
  197.3 11.9 %psum.22 = f32[256,1]{0,1:T(1,128)S(1)} all-reduce(f32[256,1]{0,1:T(1,128)S(1)} %bitcast.129), channel_id=1, replica_groups=mesh['section'=2,'seq'=4,'mp'=4] {'mp'}, use_global_device_ids=true, to_apply=%region_3.4 | all-reduce | flops 256 | bytes 2048 | tf_op jit(solution)/shard_map/psum | solution.py:55
  209.4 2.4 collective-permute-start.5
  211.8 1.3 collective-permute-done.5
  215.6 0.8 slice_bitcast_fusion.4
  216.4 4.9 %collective-permute-start.6 = (bf16[127,1024]{1,0:T(8,128)(2,1)}, bf16[127,1024]{1,0:T(8,128)(2,1)}, u32[]{:S(2)}, u32[]{:S(2)}) collective-permute-start(bf16[127,1024]{1,0:T(8,128)(2,1)} %slice_bitcast_fusion.4), channel_id=1, source_target_pairs={{0,4},{4,8},{8,12},{1,5},{5,9},{9,13},{2,6},{6,10},{10,14},{3,7},{... | collective-permute-start | bytes 780296 | tf_op jit(solution)/shard_map/ppermute | solution.py:34
  222.5 1.3 reshape.131
  223.9 0.9 collective-permute-done.6
  224.8 1.1 maximum_bitcast_fusion.2
  225.9 15.2 %fusion.75 = bf16[1,256,1024]{2,0,1:T(2,128)(2,1)} fusion(bf16[1,383,1024]{2,1,0:T(8,128)(2,1)S(1)} %maximum_bitcast_fusion.2, f32[1,264,1024]{2,0,1:T(1,128)S(1)} %reshape.131, bf16[128,1,1024]{2,0,1:T(8,128)(2,1)S(1)} %bitcast.111), kind=kOutput, calls=%fused_computation.78 | convolution fusion | flops 67633152 | bytes 2619392 | tf_op jit(solution)/shard_map/conv_general_dilated | solution.py:39
  241.1 81.2 %all-gather.9.cloned.1.call-done = bf16[1,256,4096]{2,0,1:T(2,128)(2,1)} async-done(((bf16[1,256,1024]{2,0,1:T(2,128)(2,1)}), bf16[1,256,4096]{2,0,1:T(2,128)(2,1)}) %all-gather.9.cloned.1.call-update) | async-done | bytes 2097168 | tf_op jit(solution)/shard_map/all_gather | solution.py:72
  322.3 8.6 %fusion.50 = bf16[256,1024]{1,0:T(8,128)(2,1)S(1)} fusion(bf16[4096,1024]{1,0:T(8,128)(2,1)} %bitcast.105, bf16[1,256,4096]{2,0,1:T(2,128)(2,1)} %all-gather.9.cloned.1.call-done, bf16[256,1024]{1,0:T(8,128)(2,1)S(1)} %copy-done.7), kind=kOutput, calls=%fused_computation.66 | convolution fusion | flops 2148270080 | bytes 11534336 | tf_op jit(solution)/shard_map/dot_general | solution.py:74
  330.9 1.3 collective-permute-start.7
  332.3 1.5 collective-permute-done.7
  334.0 9.4 %psum.23 = f32[256,1]{0,1:T(1,128)S(1)} all-reduce(f32[256,1]{0,1:T(1,128)S(1)} %bitcast.125), channel_id=1, replica_groups=mesh['section'=2,'seq'=4,'mp'=4] {'mp'}, use_global_device_ids=true, to_apply=%region_5.6 | all-reduce | flops 256 | bytes 2048 | tf_op jit(solution)/shard_map/psum | solution.py:55
  343.6 3.6 collective-permute-start.8
  347.2 1.2 collective-permute-done.8
  350.9 0.8 slice_bitcast_fusion.3
  351.7 4.9 %collective-permute-start.9 = (bf16[127,1024]{1,0:T(8,128)(2,1)}, bf16[127,1024]{1,0:T(8,128)(2,1)}, u32[]{:S(2)}, u32[]{:S(2)}) collective-permute-start(bf16[127,1024]{1,0:T(8,128)(2,1)} %slice_bitcast_fusion.3), channel_id=1, source_target_pairs={{0,4},{4,8},{8,12},{1,5},{5,9},{9,13},{2,6},{6,10},{10,14},{3,7},{... | collective-permute-start | bytes 780296 | tf_op jit(solution)/shard_map/ppermute | solution.py:34
  357.8 2.4 reshape.132
  360.3 1.2 maximum_bitcast_fusion.3
  361.6 15.2 %fusion.81 = bf16[1,256,1024]{2,0,1:T(2,128)(2,1)} fusion(bf16[1,383,1024]{2,1,0:T(8,128)(2,1)S(1)} %maximum_bitcast_fusion.3, f32[1,264,1024]{2,0,1:T(1,128)S(1)} %copy-done.3, bf16[128,1,1024]{2,0,1:T(8,128)(2,1)S(1)} %bitcast.112), kind=kOutput, calls=%fused_computation.80 | convolution fusion | flops 67633152 | bytes 2619392 | tf_op jit(solution)/shard_map/conv_general_dilated | solution.py:39
  376.8 1.0 copy-done.9
  377.8 80.3 %all-gather.11.cloned.1.call-done = bf16[1,256,4096]{2,0,1:T(2,128)(2,1)} async-done(((bf16[1,256,1024]{2,0,1:T(2,128)(2,1)}), bf16[1,256,4096]{2,0,1:T(2,128)(2,1)}) %all-gather.11.cloned.1.call-update) | async-done | bytes 2097168 | tf_op jit(solution)/shard_map/all_gather | solution.py:72
  458.1 8.7 %fusion.63 = bf16[1,256,1024]{2,1,0:T(8,128)(2,1)S(1)} fusion(bf16[256,1024]{1,0:T(8,128)(2,1)S(1)} %fusion.50, bf16[4096,1024]{1,0:T(8,128)(2,1)} %bitcast.106, bf16[1,256,4096]{2,0,1:T(2,128)(2,1)} %all-gather.11.cloned.1.call-done, bf16[256,1024]{1,0:T(8,128)(2,1)S(1)} %get-tuple-element.6, pred[]{:T(512)S(6)} %eq.18), kind=kOutput, calls=%fused_computation.74 | convolution fusion | flops 2148532224 | bytes 12058625 | tf_op jit(solution)/shard_map/dot_general | solution.py:74
  466.8 1.1 maximum_bitcast_fusion
  (92 shorter events, 14.5 us)
Async XLA Ops:
  6.5 4.4 copy-start
  6.5 178.0 %all-gather.7.cloned.1.call-start = ((), (), s32[]{:S(2)}) async-start(), calls=%async_computation | async-start | bytes 5242880 | tf_op jit(solution)/shard_map/all_gather | solution.py:72
  6.5 57.5 %collective-permute-start.2 = (bf16[1,1,1024,1024]{3,2,1,0:T(8,128)(2,1)}, bf16[1,1,1024,1024]{3,2,1,0:T(8,128)(2,1)}, u32[]{:S(2)}, u32[]{:S(2)}) collective-permute-start(bf16[1,1,1024,1024]{3,2,1,0:T(8,128)(2,1)} %bitcast.107), channel_id=1, source_target_pairs={{0,4},{4,0},{8,12},{12,8},{1,5},{5,1},{9,13},{13,9},{2,6},{6,2},{1... | collective-permute-start | bytes 6291464 | tf_op jit(solution)/shard_map/ppermute | solution.py:20
  11.0 15.4 %copy-start.14 = (bf16[1,3,7,1024]{3,2,1,0:T(8,128)(2,1)S(1)}, bf16[1,3,7,1024]{3,2,1,0:T(8,128)(2,1)}, u32[]{:S(2)}) copy-start(bf16[1,3,7,1024]{3,2,1,0:T(8,128)(2,1)} %param.9) | copy-start | bytes 129028
  11.5 15.6 %copy-start.10 = (bf16[1,128,1024]{2,1,0:T(8,128)(2,1)S(1)}, bf16[1,128,1024]{2,1,0:T(8,128)(2,1)}, u32[]{:S(2)}) copy-start(bf16[1,128,1024]{2,1,0:T(8,128)(2,1)} %param.10) | copy-start | bytes 786436
  23.9 31.1 %collective-permute-start = (bf16[6,1024]{1,0:T(8,128)(2,1)S(1)}, bf16[6,1024]{1,0:T(8,128)(2,1)S(1)}, u32[]{:S(2)}, u32[]{:S(2)}) collective-permute-start(bf16[6,1024]{1,0:T(8,128)(2,1)S(1)} %slice.84), channel_id=1, source_target_pairs={{0,4},{4,8},{8,12},{1,5},{5,9},{9,13},{2,6},{6,10},{10,14},{3,7},{... | collective-permute-start | bytes 36872 | tf_op jit(solution)/shard_map/ppermute | solution.py:34
  55.1 0.7 copy-start.15
  58.4 17.4 %collective-permute-start.1 = (bf16[127,1024]{1,0:T(8,128)(2,1)}, bf16[127,1024]{1,0:T(8,128)(2,1)}, u32[]{:S(2)}, u32[]{:S(2)}) collective-permute-start(bf16[127,1024]{1,0:T(8,128)(2,1)} %slice_bitcast_fusion.5), channel_id=1, source_target_pairs={{0,4},{4,8},{8,12},{1,5},{5,9},{9,13},{2,6},{6,10},{10,14},{3,7},{... | collective-permute-start | bytes 780296 | tf_op jit(solution)/shard_map/ppermute | solution.py:34
  63.5 1.6 copy-start.2
  72.0 91.6 %collective-permute-start.3 = (bf16[2,1,1024,1024]{3,2,0,1:T(8,128)(2,1)}, bf16[2,1,1024,1024]{3,2,0,1:T(8,128)(2,1)}, u32[]{:S(2)}, u32[]{:S(2)}) collective-permute-start(bf16[2,1,1024,1024]{3,2,0,1:T(8,128)(2,1)} %get-tuple-element.10), channel_id=1, source_target_pairs={{0,8},{4,12},{8,0},{12,4},{1,9},{5,13},{9,1},{13,5},{2,10},{6,14},... | collective-permute-start | bytes 12582920 | tf_op jit(solution)/shard_map/ppermute | solution.py:20
  75.8 1.3 copy-start.4
  75.8 1.4 copy-start.11
  92.3 229.9 %all-gather.9.cloned.1.call-start = ((), (), s32[]{:S(2)}) async-start(), calls=%async_computation.1 | async-start | bytes 5242880 | tf_op jit(solution)/shard_map/all_gather | solution.py:72
  193.1 4.1 copy-start.8
  193.1 2.8 collective-permute-start.4
  197.3 15.8 %copy-start.6 = (bf16[256,1024]{1,0:T(8,128)(2,1)}, bf16[256,1024]{1,0:T(8,128)(2,1)S(1)}, u32[]{:S(2)}) copy-start(bf16[256,1024]{1,0:T(8,128)(2,1)S(1)} %get-tuple-element.8) | copy-start | bytes 1572868
  209.4 3.7 collective-permute-start.5
  216.4 8.4 %collective-permute-start.6 = (bf16[127,1024]{1,0:T(8,128)(2,1)}, bf16[127,1024]{1,0:T(8,128)(2,1)}, u32[]{:S(2)}, u32[]{:S(2)}) collective-permute-start(bf16[127,1024]{1,0:T(8,128)(2,1)} %slice_bitcast_fusion.4), channel_id=1, source_target_pairs={{0,4},{4,8},{8,12},{1,5},{5,9},{9,13},{2,6},{6,10},{10,14},{3,7},{... | collective-permute-start | bytes 780296 | tf_op jit(solution)/shard_map/ppermute | solution.py:34
  223.8 2.0 copy-start.12
  225.9 96.4 %copy-start.7 = (bf16[256,1024]{1,0:T(8,128)(2,1)S(1)}, bf16[256,1024]{1,0:T(8,128)(2,1)}, u32[]{:S(2)}) copy-start(bf16[256,1024]{1,0:T(8,128)(2,1)} %copy-done.6) | copy-start | bytes 1572868
  241.1 92.7 %copy-start.5 = (bf16[256,1024]{1,0:T(8,128)(2,1)S(1)}, bf16[256,1024]{1,0:T(8,128)(2,1)}, u32[]{:S(2)}) copy-start(bf16[256,1024]{1,0:T(8,128)(2,1)} %get-tuple-element.18) | copy-start | bytes 1572868
  241.1 217.0 %all-gather.11.cloned.1.call-start = ((), (), s32[]{:S(2)}) async-start(), calls=%async_computation.2 | async-start | bytes 5242880 | tf_op jit(solution)/shard_map/all_gather | solution.py:72
  330.9 2.8 collective-permute-start.7
  343.6 4.8 %collective-permute-start.8 = (bf16[6,1024]{1,0:T(8,128)(2,1)S(1)}, bf16[6,1024]{1,0:T(8,128)(2,1)S(1)}, u32[]{:S(2)}, u32[]{:S(2)}) collective-permute-start(bf16[6,1024]{1,0:T(8,128)(2,1)S(1)} %slice.94), channel_id=1, source_target_pairs={{0,4},{4,8},{8,12},{1,5},{5,9},{9,13},{2,6},{6,10},{10,14},{3,7},{... | collective-permute-start | bytes 36872 | tf_op jit(solution)/shard_map/ppermute | solution.py:34
  351.7 8.6 %collective-permute-start.9 = (bf16[127,1024]{1,0:T(8,128)(2,1)}, bf16[127,1024]{1,0:T(8,128)(2,1)}, u32[]{:S(2)}, u32[]{:S(2)}) collective-permute-start(bf16[127,1024]{1,0:T(8,128)(2,1)} %slice_bitcast_fusion.3), channel_id=1, source_target_pairs={{0,4},{4,8},{8,12},{1,5},{5,9},{9,13},{2,6},{6,10},{10,14},{3,7},{... | collective-permute-start | bytes 780296 | tf_op jit(solution)/shard_map/ppermute | solution.py:34
  360.2 1.3 copy-start.3
  360.2 1.4 copy-start.13
  376.7 1.0 copy-start.9
  458.1 9.8 %copy-start.1 = (bf16[512,1024]{1,0:T(8,128)(2,1)S(1)}, bf16[512,1024]{1,0:T(8,128)(2,1)}, u32[]{:S(2)}) copy-start(bf16[512,1024]{1,0:T(8,128)(2,1)} %param.7) | copy-start | bytes 3145732
Sparse Core Ops, SparseCore 0:
  92.5 80.7 all-gather.6
  241.2 81.0 all-gather.8
  376.9 81.1 all-gather.10
